TPU v7x, 32 devices: a whole 2x2x4 slice. The times are simulated.
32 devices in a mesh: segment: 4 (over z), tok: 4 (over y, x), mp: 2 (over core).
Axes of the slice: x: 2, y: 2, z: 4, core: 2. Of those that a mesh axis runs over, the one named last changes fastest.
Arguments:
- out_cotangent: bfloat16 [4, 512, 4096], P('segment', 'tok', 'mp'), may hold values from -6 to 6
- block_output: bfloat16 [4, 512, 4096], P('segment', 'tok', 'mp'), may hold values from -6 to 6
- router_logits: float32 [4, 512], P('segment', 'tok'), may hold values from -8 to 8
- keep_flags: int32 [4, 512], P('segment', 'tok'), may hold values from 0 to 1, as said below
- router_weight: float32 [4, 4096], P('segment', 'mp'), may hold values from -0.09375 to 0.09375
- activated: bfloat16 [4, 64, 14336], P('segment', None, 'tok'), may hold values from -4 to 4
Outputs:
- cotangent_received: bfloat16 [4, 512, 4096], P('segment', 'tok', 'mp')
- grad_out: bfloat16 [4, 4096, 14336], P('segment', 'mp', 'tok')
Inputs may be any that keep to these rules, and one draw needn't show every extreme that they name: `keep_flags`: in every segment each aligned block of 128 tokens (one device of a group) holds at most 48 active tokens, some block holds exactly 48, and the segment holds exactly 64 active tokens.
All inputs are finite; a program needn't handle non-finite values.
Results may differ from a plain program's by a relative error of at most 0.0049.
Values may be sent and summed in bfloat16 or wider, within the bound.
No kernel may reach another device: no remote copies, remote signals or barrier semaphores. Data moves between devices by JAX's collectives and lax.ppermute only.
A program may use at most 64 MiB of HBM per device.

v0:
```python
import jax
import jax.numpy as jnp
from jax import lax
from jax.sharding import PartitionSpec as P

CAP = 48


def shifted(value, axis, by):
    devices = lax.axis_size(axis)
    pairs = [(i, i + by) for i in range(devices) if 0 <= i + by < devices]
    return lax.ppermute(value, axis, pairs)


def per_device(out_cotangent, block_output, router_logits, keep_flags, router_weight, activated):
    cotangent = out_cotangent[0]
    output = block_output[0]
    logits = router_logits[0]
    keep_row = keep_flags[0]
    router_row = router_weight[0]
    stored = activated[0]
    dy_float = cotangent.astype(jnp.float32)
    gate_value = jax.nn.sigmoid(logits)
    gate_part = jnp.sum(dy_float * output.astype(jnp.float32), axis=1)
    grad_gate = lax.psum(gate_part, "mp")
    grad_score = keep_row.astype(jnp.float32) * grad_gate * gate_value * (1.0 - gate_value)
    dx_tokens = (dy_float + grad_score[:, None] * router_row[None, :]).astype(jnp.bfloat16)
    received = shifted(dx_tokens[None], "segment", -1)
    dz_tokens = (gate_value[:, None] * dy_float).astype(jnp.bfloat16)
    position = jnp.cumsum(keep_row) - 1
    live_count = jnp.sum(keep_row)
    slot_index = jnp.arange(CAP, dtype=jnp.int32)
    chooser = ((position[None, :] == slot_index[:, None]) & (keep_row[None, :] > 0)).astype(
        jnp.bfloat16
    )
    dz_rows = jnp.dot(chooser, dz_tokens, preferred_element_type=jnp.float32).astype(jnp.bfloat16)
    every_count = lax.all_gather(live_count[None], "tok", axis=0, tiled=True)
    offsets = jnp.cumsum(every_count) - every_count
    rank_table = offsets[:, None] + slot_index[None, :]
    live_table = (slot_index[None, :] < every_count[:, None]).reshape(-1)
    safe_rank = jnp.where(live_table, rank_table.reshape(-1), 0)
    aligned = jnp.where(live_table[:, None], jnp.take(stored, safe_rank, axis=0), 0)
    all_rows = lax.all_gather(dz_rows, "tok", axis=0, tiled=True)
    gradient = lax.dot_general(
        all_rows, aligned, (((0,), (0,)), ((), ())), preferred_element_type=jnp.float32
    )
    return (received, gradient[None].astype(jnp.bfloat16))


def solution(mesh):
    in_specs = (
        P("segment", "tok", "mp"),
        P("segment", "tok", "mp"),
        P("segment", "tok"),
        P("segment", "tok"),
        P("segment", "mp"),
        P("segment", None, "tok"),
    )
    out_specs = (P("segment", "tok", "mp"), P("segment", "mp", "tok"))
    return jax.shard_map(
        per_device, mesh=mesh, in_specs=in_specs, out_specs=out_specs, check_vma=False
    )
```

profile of v0, /device:TPU:0, one launch (start us, length us, event | category | flops | bytes accessed | tf_op | source)
XLA Modules:
  0.0 43.3 jit_solution(16967838212012355003)
XLA Ops:
  0.6 0.0 copy-start
  0.6 0.0 copy-start.3
  0.7 0.0 copy-start.1
  0.7 0.0 copy-start.2
  0.7 1.5 %fusion.7 = f32[128]{0:T(128)S(1)} fusion(bf16[1,128,2048]{2,1,0:T(8,128)(2,1)} %param.6, bf16[1,128,2048]{2,1,0:T(8,128)(2,1)} %param.7), kind=kLoop, calls=%fused_computation.12 | loop fusion | flops 1048448 | bytes 1049088 | tf_op jit(solution)/shard_map/reduce_sum | solution.py:24
  2.2 2.6 %psum.7 = f32[128]{0:T(128)S(1)} all-reduce(f32[128]{0:T(128)S(1)} %fusion.7), channel_id=1, replica_groups=mesh['segment'=4,'tok'=4,'mp'=2] {'mp'}, use_global_device_ids=true, to_apply=%region_1.0 | all-reduce | flops 128 | bytes 1024 | tf_op jit(solution)/shard_map/psum | solution.py:25
  4.8 0.7 %fusion.19 = (f32[128]{0:T(128)S(1)}, f32[128]{0:T(128)S(1)}) fusion(f32[128]{0:T(128)S(1)} %psum.7, s32[1,128]{1,0:T(1,128)} %param.9, f32[1,128]{1,0:T(1,128)} %param.8), kind=kLoop, calls=%fused_computation.34 | loop fusion | flops 1024 | bytes 2560 | tf_op jit(solution)/shard_map/mul | solution.py:26
  5.5 0.0 copy-done.1
  5.5 1.7 %fusion.9 = bf16[1,128,2048]{2,1,0:T(8,128)(2,1)} fusion(bf16[1,128,2048]{2,1,0:T(8,128)(2,1)S(1)} %copy-done.1, f32[2048]{0:T(1024)} %bitcast.38, f32[128]{0:T(128)S(1)} %get-tuple-element.2), kind=kLoop, calls=%fused_computation.14 | loop fusion | flops 1048576 | bytes 1057280 | tf_op jit(solution)/shard_map/convert_element_type | solution.py:27
  7.2 1.3 %collective-permute-start = (bf16[1,128,2048]{2,1,0:T(8,128)(2,1)}, bf16[1,128,2048]{2,1,0:T(8,128)(2,1)S(1)}, u32[]{:S(2)}, u32[]{:S(2)}) collective-permute-start(bf16[1,128,2048]{2,1,0:T(8,128)(2,1)} %fusion.9), channel_id=1, source_target_pairs={{8,0},{16,8},{24,16},{9,1},{17,9},{25,17},{10,2},{18,10},{26,18},{... | collective-permute-start | bytes 1572872 | tf_op jit(solution)/shard_map/ppermute | solution.py:12
  8.5 0.0 copy-done.2
  8.5 0.6 %reduce_sum.19 = s32[]{:T(128)} reduce(s32[1,128]{1,0:T(1,128)S(1)} %copy-done.2, s32[]{:T(128)} %constant.27.clone.1), dimensions={0,1}, to_apply=%region_3.4 | reduce | flops 127 | bytes 520 | tf_op jit(solution)/shard_map/reduce_sum | solution.py:31
  9.1 0.0 copy-done.3
  9.1 0.7 %dynamic-slice = u32[1]{0:T(128)} dynamic-slice(u32[32]{0:T(128)S(1)} %copy-done.3, u32[]{:T(128)S(6)} %add.75), dynamic_slice_sizes={1} | dynamic-slice | bytes 12
  9.8 1.4 %dynamic-update-slice = s32[4]{0:T(128)S(1)} dynamic-update-slice(s32[4]{0:T(128)S(1)} %broadcast.108, s32[1]{0:T(128)} %bitcast.7, u32[]{:T(128)} %bitcast.8) | dynamic-update-slice | bytes 12
  11.2 8.7 %all-reduce = s32[4]{0:T(128)S(1)} all-reduce(s32[4]{0:T(128)S(1)} %dynamic-update-slice), channel_id=1, replica_groups=mesh['segment'=4,'tok'=4,'mp'=2] {'tok'}, use_global_device_ids=true, to_apply=%add | all-reduce | flops 4 | bytes 32
  19.9 0.1 iota_compare_fusion.1
  20.0 0.2 reduce-window.18
  20.2 0.1 iota_add_fusion
  20.3 0.1 add.70
  20.4 0.1 lt.52
  20.5 0.1 select_n.45
  20.6 0.1 copy.9
  20.7 0.2 reduce-window.17
  20.8 0.1 add_reduce_fusion
  20.9 0.3 convolution_convert_fusion.1
  21.3 12.1 %all_gather.6 = bf16[192,2048]{1,0:T(8,128)(2,1)S(1)} all-gather(bf16[48,2048]{1,0:T(8,128)(2,1)S(1)} %convolution_convert_fusion.1), channel_id=1, replica_groups=mesh['segment'=4,'tok'=4,'mp'=2] {'tok'}, dimensions={0}, use_global_device_ids=true | all-gather | bytes 983040 | tf_op jit(solution)/shard_map/all_gather | solution.py:43
  33.4 0.0 copy-done
  33.4 1.4 %gather_fusion = bf16[192,3584]{1,0:T(8,128)(2,1)S(1)} fusion(bf16[64,3584]{1,0:T(8,128)(2,1)S(1)} %bitcast.37, s32[1024]{0:T(1024)S(1)} %pad_clamp_fusion), kind=kCustom, calls=%fused_computation | custom fusion | bytes 2753280 | tf_op jit(solution)/shard_map/jit(_take)/gather | solution.py:42
  34.8 7.7 %fusion = bf16[1,2048,3584]{2,1,0:T(8,128)(2,1)} fusion(bf16[192,2048]{1,0:T(8,128)(2,1)S(1)} %all_gather.6, bf16[192,3584]{1,0:T(8,128)(2,1)S(1)} %gather_fusion, pred[192]{0:T(512)(128)(4,1)S(1)} %compare_and_fusion, pred[192]{0:T(512)(128)(4,1)S(1)} %lt.52), kind=kOutput, calls=%fused_computation.2 | convolution fusion | flops 2827288576 | bytes 16843136 | tf_op jit(solution)/shard_map/dot_general | solution.py:44
  42.5 0.0 collective-permute-done
  42.5 0.8 %copy.12 = bf16[1,128,2048]{2,1,0:T(8,128)(2,1)} copy(bf16[1,128,2048]{2,1,0:T(8,128)(2,1)S(1)} %collective-permute-done) | data formatting | bytes 1048576
  (6 shorter events, 0.0 us)
Async XLA Ops:
  0.6 32.8 %copy-start = (bf16[1,64,3584]{2,1,0:T(8,128)(2,1)S(1)}, bf16[1,64,3584]{2,1,0:T(8,128)(2,1)}, u32[]{:S(2)}) copy-start(bf16[1,64,3584]{2,1,0:T(8,128)(2,1)} %param.11) | copy-start | bytes 1376260
  0.6 8.5 %copy-start.3 = (u32[32]{0:T(128)S(1)}, u32[32]{0:T(128)}, u32[]{:S(2)}) copy-start(u32[32]{0:T(128)} %constant.41) | copy-start | bytes 388
  0.7 4.8 %copy-start.1 = (bf16[1,128,2048]{2,1,0:T(8,128)(2,1)S(1)}, bf16[1,128,2048]{2,1,0:T(8,128)(2,1)}, u32[]{:S(2)}) copy-start(bf16[1,128,2048]{2,1,0:T(8,128)(2,1)} %param.6) | copy-start | bytes 1572868
  0.7 7.8 %copy-start.2 = (s32[1,128]{1,0:T(1,128)S(1)}, s32[1,128]{1,0:T(1,128)}, u32[]{:S(2)}) copy-start(s32[1,128]{1,0:T(1,128)} %param.9) | copy-start | bytes 1540
  7.2 35.3 %collective-permute-start = (bf16[1,128,2048]{2,1,0:T(8,128)(2,1)}, bf16[1,128,2048]{2,1,0:T(8,128)(2,1)S(1)}, u32[]{:S(2)}, u32[]{:S(2)}) collective-permute-start(bf16[1,128,2048]{2,1,0:T(8,128)(2,1)} %fusion.9), channel_id=1, source_target_pairs={{8,0},{16,8},{24,16},{9,1},{17,9},{25,17},{10,2},{18,10},{26,18},{... | collective-permute-start | bytes 1572872 | tf_op jit(solution)/shard_map/ppermute | solution.py:12
where the time goes:
time: 43.6 us; the launch traced here: 43.3 us
  blocking collectives  23.5 us (54%)
  matrix products  7.99 us (18%)
  other arithmetic  5.14 us (12%)
  local copies, waits for them, and re-layouts  4.71 us (11%)
  starting transfers between devices  1.28 us (3%)
  between operations  0.73 us (2%)
    all_gather x1, blocking collectives, per_device(): all_rows = lax.all_gather(dz_rows, 'tok', axis=0, tiled=True)  12.1 us
    unnamed x1, blocking collectives  8.72 us
    dot_general x1, matrix products, per_device(): lax.dot_general(all_rows, aligned, (((0,), (0,)), ((), ())), preferred_el...  7.68 us
    unnamed x12, local copies, waits for them, and re-layouts  2.93 us
    psum x1, blocking collectives, per_device(): grad_gate = lax.psum(gate_part, 'mp')  2.62 us
    convert_element_type x1, other arithmetic, per_device(): (dy_float + grad_score[:, None] * router_row[None, :]).astype(jnp.bfloat16)  1.69 us
    reduce_sum x1, other arithmetic, per_device(): gate_part = jnp.sum(dy_float * output.astype(jnp.float32), axis=1)  1.5 us
    gather x1, local copies, waits for them, and re-layouts, per_device(): jnp.take(stored, safe_rank, axis=0)  1.42 us
  transfers between devices with their start and end apart: 1, of which 0 were waited for; matrix products, arithmetic and copies ran while one was open for 30% of the time, Pallas kernels for 0%

commit v1 on v0

v1 whole, which is shorter than its diff:
```python
import functools

import jax
import jax.numpy as jnp
from jax import lax
from jax.experimental import pallas as pl
from jax.experimental.pallas import tpu as pltpu
from jax.sharding import PartitionSpec as P


CAP = 48
LANES = 128
PIECES = 2
BLOCK = 128
LEFT = 4
MIB = 1024 * 1024

VMEM = pl.BlockSpec(memory_space=pltpu.VMEM)
ANY = pl.BlockSpec(memory_space=pl.ANY)
HBM = pl.BlockSpec(memory_space=pltpu.HBM)


def widths_of(features):
    first = features * 5 // 8 // BLOCK * BLOCK
    return [first, features - first]


def prepare_kernel(widths, cot_hbm, out_hbm, logit_hbm, keep_hbm, weight_hbm, stored_hbm, *refs):
    rows_refs = refs[: len(widths)]
    score_ref, weight_ref, stored_ref, cot_ref, out_ref, logit_ref, keep_ref, sems = refs[
        len(widths) :
    ]
    pairs = [
        (logit_hbm, logit_ref),
        (keep_hbm, keep_ref),
        (cot_hbm, cot_ref),
        (out_hbm, out_ref),
        (weight_hbm, weight_ref),
        (stored_hbm, stored_ref),
    ]
    copies = [
        pltpu.make_async_copy(source, target, sems.at[index])
        for index, (source, target) in enumerate(pairs)
    ]
    for copy in copies:
        copy.start()
    tokens = cot_ref.shape[0]
    upper = (
        lax.broadcasted_iota(jnp.int32, (tokens, tokens), 0)
        <= lax.broadcasted_iota(jnp.int32, (tokens, tokens), 1)
    ).astype(jnp.float32).astype(jnp.bfloat16)
    copies[0].wait()
    copies[1].wait()
    keep = keep_ref[...]
    gate = jax.nn.sigmoid(logit_ref[...])
    keep_half = jnp.broadcast_to(keep.astype(jnp.float32), (16, tokens)).astype(jnp.bfloat16)
    rank = jnp.dot(keep_half, upper, preferred_element_type=jnp.float32)[:1]
    slot = lax.broadcasted_iota(jnp.int32, (CAP, tokens), 0) + 1
    chosen = (rank.astype(jnp.int32) == slot) & (keep > 0)
    gate_column = jnp.sum(jnp.where(chosen, gate, 0.0), axis=1, keepdims=True)
    chooser = jnp.where(chosen, 1.0, 0.0).astype(jnp.bfloat16)
    count = jnp.sum(keep.astype(jnp.float32), axis=1, keepdims=True)
    copies[2].wait()
    start = 0
    for index, (ref, width) in enumerate(zip(rows_refs, widths)):
        picked = jnp.dot(
            chooser, cot_ref[:, start : start + width], preferred_element_type=jnp.float32
        )
        ref[:, :width] = (picked * gate_column).astype(jnp.bfloat16)
        if index == 0:
            ref[:, width:] = jnp.broadcast_to(count, (CAP, LANES)).astype(jnp.bfloat16)
        start += width
    copies[3].wait()
    folded = jnp.zeros((tokens, LANES), jnp.float32)
    for start in range(0, cot_ref.shape[1], LANES):
        folded = folded + (
            cot_ref[:, start : start + LANES].astype(jnp.float32)
            * out_ref[:, start : start + LANES].astype(jnp.float32)
        )
    part = jnp.sum(folded.T, axis=0, keepdims=True)
    score_ref[...] = keep.astype(jnp.float32) * part * gate * (1.0 - gate)
    copies[4].wait()
    copies[5].wait()


def prepare(cotangent, output, logits, keep_row, weight, stored):
    widths = widths_of(cotangent.shape[1])
    return pl.pallas_call(
        functools.partial(prepare_kernel, widths),
        in_specs=[HBM] * 6,
        out_specs=[VMEM] * (len(widths) + 3),
        out_shape=[
            pltpu.VMEM((CAP, width + (LANES if index == 0 else 0)), jnp.bfloat16)
            for index, width in enumerate(widths)
        ]
        + [
            pltpu.VMEM(logits.shape, jnp.float32),
            pltpu.VMEM(weight.shape, jnp.float32),
            pltpu.VMEM(stored.shape, jnp.bfloat16),
        ],
        scratch_shapes=[
            pltpu.VMEM(cotangent.shape, jnp.bfloat16),
            pltpu.VMEM(output.shape, jnp.bfloat16),
            pltpu.VMEM(logits.shape, jnp.float32),
            pltpu.VMEM(keep_row.shape, jnp.int32),
            pltpu.SemaphoreType.DMA((6,)),
        ],
        compiler_params=pltpu.CompilerParams(vmem_limit_bytes=8 * MIB),
        name="prepare",
    )(*[
        pltpu.with_memory_space_constraint(x, pltpu.HBM)
        for x in (cotangent, output, logits, keep_row, weight, stored)
    ])


def place_of(row_refs, width, total):
    group = len(row_refs)
    me = lax.axis_index("tok")
    counts = [ref[:1, width : width + LANES].astype(jnp.float32)[:, :CAP] for ref in row_refs]
    owners = [partner(me, r, group) for r in range(group)]
    lane = lax.broadcasted_iota(jnp.int32, (total, CAP), 1)
    target = lax.broadcasted_iota(jnp.int32, (total, CAP), 0)
    places = []
    for r in range(group):
        offset = jnp.zeros_like(counts[0])
        for other in range(group):
            if other != r:
                ahead = (owners[other] < owners[r]).astype(jnp.float32)
                offset = offset + counts[other] * ahead
        place = (offset.astype(jnp.int32) + lane == target) & (lane < counts[r].astype(jnp.int32))
        places.append(jnp.where(place, 1.0, 0.0).astype(jnp.bfloat16))
    return places


def pack_rows(row_refs, places, lhs_ref):
    width = lhs_ref.shape[0]
    packed = None
    for place, ref in zip(places, row_refs):
        one = jnp.dot(place, ref[:, :width], preferred_element_type=jnp.float32)
        packed = one if packed is None else packed + one
    lhs_ref[...] = packed.T.astype(jnp.bfloat16)


def product(lhs_ref, start, stored_ref):
    return jnp.dot(
        lhs_ref[start : start + BLOCK, :], stored_ref[...], preferred_element_type=jnp.float32
    ).astype(jnp.bfloat16)


def first_gradient(widths, pieces, stored):
    width = widths[0]
    total, hidden = stored.shape
    group = len(pieces)
    sent = width - LEFT * BLOCK

    def kernel(*refs):
        row_refs = refs[:group]
        stored_ref, grad_ref, place_ref, spare_ref, lhs_ref, held_ref, sems = refs[group:]
        places = place_of(row_refs, width, total)
        for r in range(group):
            place_ref[r] = places[r]
        pack_rows(row_refs, places, lhs_ref)
        copies = []
        for index, start in enumerate(range(0, sent, BLOCK)):
            held_ref[start : start + BLOCK, :] = product(lhs_ref, start, stored_ref)
            copy = pltpu.make_async_copy(
                held_ref.at[pl.ds(start, BLOCK)],
                grad_ref.at[pl.ds(start, BLOCK)],
                sems.at[index],
            )
            copy.start()
            copies.append(copy)
        for start in range(sent, width, BLOCK):
            spare_ref[start - sent : start - sent + BLOCK, :] = product(lhs_ref, start, stored_ref)
        for copy in copies:
            copy.wait()

    return pl.pallas_call(
        kernel,
        in_specs=[VMEM] * (group + 1),
        out_specs=[ANY, VMEM, VMEM],
        out_shape=[
            jax.ShapeDtypeStruct((sum(widths), hidden), jnp.bfloat16),
            pltpu.VMEM((group, total, CAP), jnp.bfloat16),
            pltpu.VMEM((LEFT * BLOCK, hidden), jnp.bfloat16),
        ],
        scratch_shapes=[
            pltpu.VMEM((width, total), jnp.bfloat16),
            pltpu.VMEM((sent, hidden), jnp.bfloat16),
            pltpu.SemaphoreType.DMA((sent // BLOCK,)),
        ],
        compiler_params=pltpu.CompilerParams(vmem_limit_bytes=20 * MIB),
        name="gradient0",
    )(*pieces, stored)


def second_gradient(widths, pieces, stored, gradient, place, spare):
    width = widths[1]
    base = widths[0]
    total, hidden = stored.shape
    group = len(pieces)
    left = LEFT * BLOCK

    def kernel(*refs):
        row_refs = refs[:group]
        stored_ref, place_ref, spare_ref, _, grad_ref, lhs_ref, held_ref, sems = refs[group:]
        copies = []
        for index, start in enumerate(range(0, left, BLOCK)):
            copy = pltpu.make_async_copy(
                spare_ref.at[pl.ds(start, BLOCK)],
                grad_ref.at[pl.ds(base - left + start, BLOCK)],
                sems.at[index],
            )
            copy.start()
            copies.append(copy)
        pack_rows(row_refs, [place_ref[r] for r in range(group)], lhs_ref)
        for index, start in enumerate(range(0, width, BLOCK)):
            held_ref[start : start + BLOCK, :] = product(lhs_ref, start, stored_ref)
            copy = pltpu.make_async_copy(
                held_ref.at[pl.ds(start, BLOCK)],
                grad_ref.at[pl.ds(base + start, BLOCK)],
                sems.at[LEFT + index],
            )
            copy.start()
            copies.append(copy)
        for copy in copies:
            copy.wait()

    return pl.pallas_call(
        kernel,
        in_specs=[VMEM] * (group + 3) + [ANY],
        out_specs=ANY,
        out_shape=jax.ShapeDtypeStruct((sum(widths), hidden), jnp.bfloat16),
        input_output_aliases={group + 3: 0},
        scratch_shapes=[
            pltpu.VMEM((width, total), jnp.bfloat16),
            pltpu.VMEM((width, hidden), jnp.bfloat16),
            pltpu.SemaphoreType.DMA((LEFT + width // BLOCK,)),
        ],
        compiler_params=pltpu.CompilerParams(vmem_limit_bytes=20 * MIB),
        name="gradient1",
    )(*pieces, stored, place, spare, gradient)


def partner(index, r, group):
    if group & (group - 1):
        return (index + r) % group
    return index ^ r


def per_device(out_cotangent, block_output, router_logits, keep_flags, router_weight, activated):
    cotangent = out_cotangent[0]
    stored = activated[0]
    segments = lax.axis_size("segment")
    group = lax.axis_size("tok")
    halves = lax.axis_size("mp")
    widths = widths_of(cotangent.shape[1])

    back = [(i, (i - 1) % segments) for i in range(segments)]
    came = lax.ppermute(cotangent, "segment", back)
    *rows, score_part, weight, held = prepare(
        cotangent, block_output[0], router_logits, keep_flags, router_weight, stored
    )
    pieces = []
    for index in range(PIECES):
        pieces.append(
            [rows[index]]
            + [
                lax.ppermute(rows[index], "tok", [(partner(i, r, group), i) for i in range(group)])
                for r in range(1, group)
            ]
        )
    score = score_part
    for r in range(1, halves):
        score = score + lax.ppermute(
            score_part, "mp", [(i, (i + r) % halves) for i in range(halves)]
        )
    tokens = score.shape[1]
    small = lax.ppermute(
        jnp.concatenate([score, weight], axis=1), "segment", back
    )
    gradient, place, spare = first_gradient(widths, pieces[0], held)
    gradient = second_gradient(widths, pieces[1], held, gradient, place, spare)
    received = (
        came.astype(jnp.float32) + small[0, :tokens, None] * small[:, tokens:]
    ).astype(jnp.bfloat16)
    received = jnp.where(lax.axis_index("segment") == segments - 1, 0, received)
    return (received[None], gradient[None])


def solution(mesh):
    in_specs = (
        P("segment", "tok", "mp"),
        P("segment", "tok", "mp"),
        P("segment", "tok"),
        P("segment", "tok"),
        P("segment", "mp"),
        P("segment", None, "tok"),
    )
    out_specs = (P("segment", "tok", "mp"), P("segment", "mp", "tok"))
    return jax.shard_map(
        per_device, mesh=mesh, in_specs=in_specs, out_specs=out_specs, check_vma=False
    )
```

time: 43.6 us -> 33.8 us (0.78)
  blocking collectives: 23.5 us -> 0 us
  starting transfers between devices: 1.28 us -> 12.7 us
  waiting for transfers between devices: 0.01 us -> 10.6 us
  Pallas kernels: 0 us -> 8.53 us
  matrix products: 7.99 us -> 0 us
  local copies, waits for them, and re-layouts: 4.71 us -> 0.01 us
  other arithmetic: 5.14 us -> 1.04 us
    all_gather x1 -> x0, blocking collectives: 12.1 us -> none  [per_device(): all_rows = lax.all_gather(dz_rows, 'tok', axis=0, tiled=True)]
    ppermute x1 -> x9, starting transfers between devices: 1.28 us -> 12.7 us  [the longest x6 8.04 us: per_device(): lax.ppermute(rows[index], 'tok', [(partner(i, r, group), i) for i in rang...]
    ppermute x1 -> x9, waiting for transfers between devices: 0.01 us -> 10.6 us  [the longest x1 10.6 us: per_device(): lax.ppermute(jnp.concatenate([score, weight], axis=1), 'segment', back)]
    unnamed x1 -> x0, blocking collectives: 8.72 us -> none
    pallas_call x0 -> x3, Pallas kernels: none -> 8.53 us  [the longest x1 3.64 us: second_gradient(): pl.pallas_call(kernel, in_specs=[VMEM] * (group + 3) + [ANY], out_specs=A...]
    dot_general x2 -> x0, matrix products: 7.99 us -> none  [the longest x1 7.68 us: per_device(): lax.dot_general(all_rows, aligned, (((0,), (0,)), ((), ())), preferred_el...]
    unnamed x12 -> x0, local copies, waits for them, and re-layouts: 2.93 us -> none
    psum x1 -> x0, blocking collectives: 2.62 us -> none  [per_device(): grad_gate = lax.psum(gate_part, 'mp')]
  transfers between devices with their start and end apart: 1 -> 9, of which waited for: 0 -> 1; matrix products, arithmetic and copies ran while one was open for 30% -> 0% of each run, Pallas kernels for 0% -> 21%
where the time goes in v1:
time: 33.8 us; the launch traced here: 33.6 us
  starting transfers between devices  12.7 us (38%)
  waiting for transfers between devices  10.6 us (31%)
  Pallas kernels  8.53 us (25%)
  other arithmetic  1.04 us (3%)
  between operations  0.7 us (2%)
    ppermute x1, waiting for transfers between devices, per_device(): lax.ppermute(jnp.concatenate([score, weight], axis=1), 'segment', back)  10.6 us
    ppermute x6, starting transfers between devices, per_device(): lax.ppermute(rows[index], 'tok', [(partner(i, r, group), i) for i in rang...  8.04 us
    pallas_call x1, Pallas kernels, second_gradient(): pl.pallas_call(kernel, in_specs=[VMEM] * (group + 3) + [ANY], out_specs=A...  3.64 us
    ppermute x1, starting transfers between devices, per_device(): came = lax.ppermute(cotangent, 'segment', back)  3.6 us
    pallas_call x1, Pallas kernels, first_gradient(): pl.pallas_call(kernel, in_specs=[VMEM] * (group + 1), out_specs=[ANY, VME...  3.31 us
    pallas_call x1, Pallas kernels, prepare(): pl.pallas_call(functools.partial(prepare_kernel, widths), in_specs=[HBM]...  1.58 us
    broadcast_in_dim x1, other arithmetic, per_device(): return (received[None], gradient[None])  1.03 us
  transfers between devices with their start and end apart: 9, of which 1 were waited for; matrix products, arithmetic and copies ran while one was open for 0% of the time, Pallas kernels for 21%

profile of v1, /device:TPU:0, one launch (start us, length us, event | category | flops | bytes accessed | tf_op | source)
XLA Modules:
  0.0 33.6 jit_solution(2558145147127499523)
XLA Ops:
  0.6 1.6 %prepare.1 = (bf16[48,1408]{1,0:T(8,128)(2,1)S(1)}, bf16[48,768]{1,0:T(8,128)(2,1)S(1)}, f32[1,128]{1,0:T(1,128)S(1)}, f32[1,2048]{1,0:T(1,128)S(1)}, bf16[64,3584]{1,0:T(8,128)(2,1)S(1)}) custom-call(bf16[128,2048]{1,0:T(8,128)(2,1)} %bitcast.11, bf16[128,2048]{1,0:T(8,128)(2,1)} %bitcast.10, f32[1,128]{1,0:T(1,128)} %logit_hbm.1, s32[1,128]{1,0:T(1,128)} %keep_hbm.1, ...), custom_call_target="tpu_custom_call" | custom-call | tf_op jit(solution)/shard_map/prepare/pallas_call | solution.py:88
  2.2 0.6 %collective-permute-start.1 = (f32[1,128]{1,0:T(1,128)S(1)}, f32[1,128]{1,0:T(1,128)S(1)}, u32[]{:S(2)}, u32[]{:S(2)}) collective-permute-start(f32[1,128]{1,0:T(1,128)S(1)} %get-tuple-element.10), channel_id=1, source_target_pairs={{0,1},{1,0},{2,3},{3,2},{4,5},{5,4},{6,7},{7,6},{8,9},{9,8},{10,11... | collective-permute-start | bytes 1544 | tf_op jit(solution)/shard_map/ppermute | solution.py:275
  2.8 2.5 %collective-permute-start.6 = (bf16[48,1408]{1,0:T(8,128)(2,1)S(1)}, bf16[48,1408]{1,0:T(8,128)(2,1)S(1)}, u32[]{:S(2)}, u32[]{:S(2)}) collective-permute-start(bf16[48,1408]{1,0:T(8,128)(2,1)S(1)} %get-tuple-element.14.refs_0_), channel_id=1, source_target_pairs={{2,0},{0,2},{6,4},{4,6},{3,1},{1,3},{7,5},{5,7},{10,8},{8,10},{14,... | collective-permute-start | bytes 405512 | tf_op jit(solution)/shard_map/ppermute | solution.py:269
  5.3 1.5 %collective-permute-start.7 = (bf16[48,1408]{1,0:T(8,128)(2,1)S(1)}, bf16[48,1408]{1,0:T(8,128)(2,1)S(1)}, u32[]{:S(2)}, u32[]{:S(2)}) collective-permute-start(bf16[48,1408]{1,0:T(8,128)(2,1)S(1)} %get-tuple-element.14.refs_0_), channel_id=1, source_target_pairs={{4,0},{6,2},{0,4},{2,6},{5,1},{7,3},{1,5},{3,7},{12,8},{14,10},{8,... | collective-permute-start | bytes 405512 | tf_op jit(solution)/shard_map/ppermute | solution.py:269
  6.8 3.6 %collective-permute-start = (bf16[128,2048]{1,0:T(8,128)(2,1)}, bf16[128,2048]{1,0:T(8,128)(2,1)S(1)}, u32[]{:S(2)}, u32[]{:S(2)}) collective-permute-start(bf16[128,2048]{1,0:T(8,128)(2,1)} %bitcast.12), channel_id=1, source_target_pairs={{0,24},{8,0},{16,8},{24,16},{1,25},{9,1},{17,9},{25,17},{2,26},{10... | collective-permute-start | bytes 1572872 | tf_op jit(solution)/shard_map/ppermute | solution.py:260
  10.5 0.0 collective-permute-done.1
  10.5 0.5 %collective-permute-start.2 = (f32[1,2176]{1,0:T(1,128)S(1)}, f32[1,2176]{1,0:T(1,128)S(1)}, u32[]{:S(2)}, u32[]{:S(2)}) collective-permute-start(f32[1,2176]{1,0:T(1,128)S(1)} %pad_maximum_fusion), channel_id=1, source_target_pairs={{0,24},{8,0},{16,8},{24,16},{1,25},{9,1},{17,9},{25,17},{2,26},{10... | collective-permute-start | bytes 26120 | tf_op jit(solution)/shard_map/ppermute | solution.py:279
  11.0 0.5 %collective-permute-start.8 = (bf16[48,1408]{1,0:T(8,128)(2,1)S(1)}, bf16[48,1408]{1,0:T(8,128)(2,1)S(1)}, u32[]{:S(2)}, u32[]{:S(2)}) collective-permute-start(bf16[48,1408]{1,0:T(8,128)(2,1)S(1)} %get-tuple-element.14.refs_0_), channel_id=1, source_target_pairs={{6,0},{4,2},{2,4},{0,6},{7,1},{5,3},{3,5},{1,7},{14,8},{12,10},{10... | collective-permute-start | bytes 405512 | tf_op jit(solution)/shard_map/ppermute | solution.py:269
  11.5 10.6 %collective-permute-done.2 = f32[1,2176]{1,0:T(1,128)S(1)} collective-permute-done((f32[1,2176]{1,0:T(1,128)S(1)}, f32[1,2176]{1,0:T(1,128)S(1)}, u32[]{:S(2)}, u32[]{:S(2)}) %collective-permute-start.2) | collective-permute-done | bytes 8736 | tf_op jit(solution)/shard_map/ppermute | solution.py:279
  22.1 0.5 %collective-permute-start.3 = (bf16[48,768]{1,0:T(8,128)(2,1)S(1)}, bf16[48,768]{1,0:T(8,128)(2,1)S(1)}, u32[]{:S(2)}, u32[]{:S(2)}) collective-permute-start(bf16[48,768]{1,0:T(8,128)(2,1)S(1)} %get-tuple-element.12.refs_0_), channel_id=1, source_target_pairs={{2,0},{0,2},{6,4},{4,6},{3,1},{1,3},{7,5},{5,7},{10,8},{8,10},{14,... | collective-permute-start | bytes 221192 | tf_op jit(solution)/shard_map/ppermute | solution.py:269
  22.6 0.0 collective-permute-done.6.refs_1_
  22.6 0.5 %collective-permute-start.4 = (bf16[48,768]{1,0:T(8,128)(2,1)S(1)}, bf16[48,768]{1,0:T(8,128)(2,1)S(1)}, u32[]{:S(2)}, u32[]{:S(2)}) collective-permute-start(bf16[48,768]{1,0:T(8,128)(2,1)S(1)} %get-tuple-element.12.refs_0_), channel_id=1, source_target_pairs={{4,0},{6,2},{0,4},{2,6},{5,1},{7,3},{1,5},{3,7},{12,8},{14,10},{8,... | collective-permute-start | bytes 221192 | tf_op jit(solution)/shard_map/ppermute | solution.py:269
  23.1 0.0 collective-permute-done.7.refs_2_
  23.1 2.4 %collective-permute-start.5 = (bf16[48,768]{1,0:T(8,128)(2,1)S(1)}, bf16[48,768]{1,0:T(8,128)(2,1)S(1)}, u32[]{:S(2)}, u32[]{:S(2)}) collective-permute-start(bf16[48,768]{1,0:T(8,128)(2,1)S(1)} %get-tuple-element.12.refs_0_), channel_id=1, source_target_pairs={{6,0},{4,2},{2,4},{0,6},{7,1},{5,3},{3,5},{1,7},{14,8},{12,10},{10... | collective-permute-start | bytes 221192 | tf_op jit(solution)/shard_map/ppermute | solution.py:269
  25.6 0.0 collective-permute-done.8.refs_3_
  25.6 3.3 %gradient0.1 = (bf16[2048,3584]{1,0:T(8,128)(2,1)}, bf16[4,64,48]{2,1,0:T(8,128)(2,1)S(1)}, bf16[512,3584]{1,0:T(8,128)(2,1)S(1)}) custom-call(bf16[48,1408]{1,0:T(8,128)(2,1)S(1)} %get-tuple-element.14.refs_0_, bf16[48,1408]{1,0:T(8,128)(2,1)S(1)} %collective-permute-done.6.refs_1_, bf16[48,1408]{1,0:T(8,128)(2,1)S(1)} %collective-permute-done.7.refs_2_, ...), custom_call_target="tpu_custom_call" | custom-call | tf_op jit(solution)/shard_map/gradient0/pallas_call | solution.py:178
  28.9 0.0 collective-permute-done.3.refs_1_
  28.9 0.0 collective-permute-done.4.refs_2_
  28.9 0.0 collective-permute-done.5.refs_3_
  28.9 3.6 %gradient1.1 = bf16[2048,3584]{1,0:T(8,128)(2,1)} custom-call(bf16[48,768]{1,0:T(8,128)(2,1)S(1)} %get-tuple-element.12.refs_0_, bf16[48,768]{1,0:T(8,128)(2,1)S(1)} %collective-permute-done.3.refs_1_, bf16[48,768]{1,0:T(8,128)(2,1)S(1)} %collective-permute-done.4.refs_2_, ...), custom_call_target="tpu_custom_call", output_to_operand_aliasing={{}: (7, {})} | custom-call | tf_op jit(solution)/shard_map/gradient1/pallas_call | solution.py:229
  32.6 0.0 collective-permute-done
  32.6 1.0 %fusion.1 = bf16[1,128,2048]{2,1,0:T(8,128)(2,1)} fusion(bf16[128,2048]{1,0:T(8,128)(2,1)S(1)} %collective-permute-done, f32[2048]{0:T(1024)S(1)} %bitcast.14, f32[128]{0:T(128)S(1)} %slice_bitcast_fusion, pred[]{:T(512)S(6)} %eq.3), kind=kLoop, calls=%fused_computation.2 | loop fusion | flops 1310720 | bytes 1057281 | tf_op jit(solution)/shard_map/broadcast_in_dim | solution.py:288
  (4 shorter events, 0.0 us)
Async XLA Ops:
  2.2 8.2 %collective-permute-start.1 = (f32[1,128]{1,0:T(1,128)S(1)}, f32[1,128]{1,0:T(1,128)S(1)}, u32[]{:S(2)}, u32[]{:S(2)}) collective-permute-start(f32[1,128]{1,0:T(1,128)S(1)} %get-tuple-element.10), channel_id=1, source_target_pairs={{0,1},{1,0},{2,3},{3,2},{4,5},{5,4},{6,7},{7,6},{8,9},{9,8},{10,11... | collective-permute-start | bytes 1544 | tf_op jit(solution)/shard_map/ppermute | solution.py:275
  2.8 19.8 %collective-permute-start.6 = (bf16[48,1408]{1,0:T(8,128)(2,1)S(1)}, bf16[48,1408]{1,0:T(8,128)(2,1)S(1)}, u32[]{:S(2)}, u32[]{:S(2)}) collective-permute-start(bf16[48,1408]{1,0:T(8,128)(2,1)S(1)} %get-tuple-element.14.refs_0_), channel_id=1, source_target_pairs={{2,0},{0,2},{6,4},{4,6},{3,1},{1,3},{7,5},{5,7},{10,8},{8,10},{14,... | collective-permute-start | bytes 405512 | tf_op jit(solution)/shard_map/ppermute | solution.py:269
  5.3 17.8 %collective-permute-start.7 = (bf16[48,1408]{1,0:T(8,128)(2,1)S(1)}, bf16[48,1408]{1,0:T(8,128)(2,1)S(1)}, u32[]{:S(2)}, u32[]{:S(2)}) collective-permute-start(bf16[48,1408]{1,0:T(8,128)(2,1)S(1)} %get-tuple-element.14.refs_0_), channel_id=1, source_target_pairs={{4,0},{6,2},{0,4},{2,6},{5,1},{7,3},{1,5},{3,7},{12,8},{14,10},{8,... | collective-permute-start | bytes 405512 | tf_op jit(solution)/shard_map/ppermute | solution.py:269
  6.8 25.7 %collective-permute-start = (bf16[128,2048]{1,0:T(8,128)(2,1)}, bf16[128,2048]{1,0:T(8,128)(2,1)S(1)}, u32[]{:S(2)}, u32[]{:S(2)}) collective-permute-start(bf16[128,2048]{1,0:T(8,128)(2,1)} %bitcast.12), channel_id=1, source_target_pairs={{0,24},{8,0},{16,8},{24,16},{1,25},{9,1},{17,9},{25,17},{2,26},{10... | collective-permute-start | bytes 1572872 | tf_op jit(solution)/shard_map/ppermute | solution.py:260
  10.5 11.6 %collective-permute-start.2 = (f32[1,2176]{1,0:T(1,128)S(1)}, f32[1,2176]{1,0:T(1,128)S(1)}, u32[]{:S(2)}, u32[]{:S(2)}) collective-permute-start(f32[1,2176]{1,0:T(1,128)S(1)} %pad_maximum_fusion), channel_id=1, source_target_pairs={{0,24},{8,0},{16,8},{24,16},{1,25},{9,1},{17,9},{25,17},{2,26},{10... | collective-permute-start | bytes 26120 | tf_op jit(solution)/shard_map/ppermute | solution.py:279
  11.0 14.6 %collective-permute-start.8 = (bf16[48,1408]{1,0:T(8,128)(2,1)S(1)}, bf16[48,1408]{1,0:T(8,128)(2,1)S(1)}, u32[]{:S(2)}, u32[]{:S(2)}) collective-permute-start(bf16[48,1408]{1,0:T(8,128)(2,1)S(1)} %get-tuple-element.14.refs_0_), channel_id=1, source_target_pairs={{6,0},{4,2},{2,4},{0,6},{7,1},{5,3},{3,5},{1,7},{14,8},{12,10},{10... | collective-permute-start | bytes 405512 | tf_op jit(solution)/shard_map/ppermute | solution.py:269
  22.1 6.8 %collective-permute-start.3 = (bf16[48,768]{1,0:T(8,128)(2,1)S(1)}, bf16[48,768]{1,0:T(8,128)(2,1)S(1)}, u32[]{:S(2)}, u32[]{:S(2)}) collective-permute-start(bf16[48,768]{1,0:T(8,128)(2,1)S(1)} %get-tuple-element.12.refs_0_), channel_id=1, source_target_pairs={{2,0},{0,2},{6,4},{4,6},{3,1},{1,3},{7,5},{5,7},{10,8},{8,10},{14,... | collective-permute-start | bytes 221192 | tf_op jit(solution)/shard_map/ppermute | solution.py:269
  22.6 6.3 %collective-permute-start.4 = (bf16[48,768]{1,0:T(8,128)(2,1)S(1)}, bf16[48,768]{1,0:T(8,128)(2,1)S(1)}, u32[]{:S(2)}, u32[]{:S(2)}) collective-permute-start(bf16[48,768]{1,0:T(8,128)(2,1)S(1)} %get-tuple-element.12.refs_0_), channel_id=1, source_target_pairs={{4,0},{6,2},{0,4},{2,6},{5,1},{7,3},{1,5},{3,7},{12,8},{14,10},{8,... | collective-permute-start | bytes 221192 | tf_op jit(solution)/shard_map/ppermute | solution.py:269
  23.1 5.8 %collective-permute-start.5 = (bf16[48,768]{1,0:T(8,128)(2,1)S(1)}, bf16[48,768]{1,0:T(8,128)(2,1)S(1)}, u32[]{:S(2)}, u32[]{:S(2)}) collective-permute-start(bf16[48,768]{1,0:T(8,128)(2,1)S(1)} %get-tuple-element.12.refs_0_), channel_id=1, source_target_pairs={{6,0},{4,2},{2,4},{0,6},{7,1},{5,3},{3,5},{1,7},{14,8},{12,10},{10... | collective-permute-start | bytes 221192 | tf_op jit(solution)/shard_map/ppermute | solution.py:269

commit v2 on v1

v2 whole, which is shorter than its diff:
```python
import jax
import jax.numpy as jnp
from jax import lax
from jax.experimental import pallas as pl
from jax.experimental.pallas import tpu as pltpu
from jax.sharding import PartitionSpec as P


CAP = 48
LANES = 128
BLOCK = 128
FIRST = 6
LEFT = 3
MIB = 1024 * 1024

VMEM = pl.BlockSpec(memory_space=pltpu.VMEM)
ANY = pl.BlockSpec(memory_space=pl.ANY)
HBM = pl.BlockSpec(memory_space=pltpu.HBM)


def prepare_kernel(cot_hbm, out_hbm, logit_hbm, keep_hbm, weight_hbm, stored_hbm, *refs):
    rows_ref, score_ref, weight_ref, stored_ref, cot_ref, out_ref, logit_ref, keep_ref, sems = refs
    pairs = [
        (logit_hbm, logit_ref),
        (keep_hbm, keep_ref),
        (cot_hbm, cot_ref),
        (out_hbm, out_ref),
        (weight_hbm, weight_ref),
        (stored_hbm, stored_ref),
    ]
    copies = [
        pltpu.make_async_copy(source, target, sems.at[index])
        for index, (source, target) in enumerate(pairs)
    ]
    for copy in copies:
        copy.start()
    tokens = cot_ref.shape[0]
    upper = (
        lax.broadcasted_iota(jnp.int32, (tokens, tokens), 0)
        <= lax.broadcasted_iota(jnp.int32, (tokens, tokens), 1)
    ).astype(jnp.float32).astype(jnp.bfloat16)
    copies[0].wait()
    copies[1].wait()
    keep = keep_ref[...]
    gate = jax.nn.sigmoid(logit_ref[...])
    keep_half = jnp.broadcast_to(keep.astype(jnp.float32), (16, tokens)).astype(jnp.bfloat16)
    rank = jnp.dot(keep_half, upper, preferred_element_type=jnp.float32)[:1]
    slot = lax.broadcasted_iota(jnp.int32, (CAP, tokens), 0) + 1
    chosen = (rank.astype(jnp.int32) == slot) & (keep > 0)
    gate_column = jnp.sum(jnp.where(chosen, gate, 0.0), axis=1, keepdims=True)
    chooser = jnp.where(chosen, 1.0, 0.0).astype(jnp.bfloat16)
    count = jnp.sum(keep.astype(jnp.float32), axis=1, keepdims=True)
    copies[2].wait()
    width = cot_ref.shape[1]
    picked = jnp.dot(chooser, cot_ref[...], preferred_element_type=jnp.float32)
    rows_ref[:, :width] = (picked * gate_column).astype(jnp.bfloat16)
    rows_ref[:, width:] = jnp.broadcast_to(count, (CAP, LANES)).astype(jnp.bfloat16)
    copies[3].wait()
    folded = jnp.zeros((tokens, LANES), jnp.float32)
    for start in range(0, cot_ref.shape[1], LANES):
        folded = folded + (
            cot_ref[:, start : start + LANES].astype(jnp.float32)
            * out_ref[:, start : start + LANES].astype(jnp.float32)
        )
    part = jnp.sum(folded.T, axis=0, keepdims=True)
    score_ref[...] = keep.astype(jnp.float32) * part * gate * (1.0 - gate)
    copies[4].wait()
    copies[5].wait()


def prepare(cotangent, output, logits, keep_row, weight, stored):
    operands = (cotangent, output, logits, keep_row, weight, stored)
    return pl.pallas_call(
        prepare_kernel,
        in_specs=[HBM] * 6,
        out_specs=[VMEM] * 5,
        out_shape=[
            pltpu.VMEM((CAP, cotangent.shape[1] + LANES), jnp.bfloat16),
            pltpu.VMEM(logits.shape, jnp.float32),
            pltpu.VMEM(weight.shape, jnp.float32),
            pltpu.VMEM(stored.shape, jnp.bfloat16),
            pltpu.VMEM(cotangent.shape, jnp.bfloat16),
        ],
        scratch_shapes=[
            pltpu.VMEM(output.shape, jnp.bfloat16),
            pltpu.VMEM(logits.shape, jnp.float32),
            pltpu.VMEM(keep_row.shape, jnp.int32),
            pltpu.SemaphoreType.DMA((6,)),
        ],
        compiler_params=pltpu.CompilerParams(vmem_limit_bytes=8 * MIB),
        name="prepare",
    )(*[pltpu.with_memory_space_constraint(x, pltpu.HBM) for x in operands])


def input_gradient(cotangent, scores, weight):
    tokens = cotangent.shape[0]

    def kernel(cot_ref, weight_ref, *refs):
        *score_refs, dx_ref = refs
        score = score_refs[0][...]
        for ref in score_refs[1:]:
            score = score + ref[...]
        column = jnp.broadcast_to(score, (LANES, tokens)).T
        for start in range(0, cot_ref.shape[1], LANES):
            lanes = slice(start, start + LANES)
            dx_ref[:, lanes] = (
                cot_ref[:, lanes].astype(jnp.float32) + column * weight_ref[:, lanes]
            ).astype(jnp.bfloat16)

    return pl.pallas_call(
        kernel,
        in_specs=[VMEM] * (2 + len(scores)),
        out_specs=VMEM,
        out_shape=pltpu.VMEM(cotangent.shape, jnp.bfloat16),
        compiler_params=pltpu.CompilerParams(vmem_limit_bytes=4 * MIB),
        name="input_gradient",
    )(cotangent, weight, *scores)


def light_rows(total):
    return min(CAP, total - CAP)


def mask_of(phase, half, phases):
    return 1 << ((phase + half) % phases)


def widths_of(features):
    first = features * FIRST // 16 // BLOCK * BLOCK
    return first, features - first


def merge(own, came, light, split):
    rows, width = own.shape
    heavy = CAP - light
    lights = rows - heavy
    features = width - LANES
    if split:
        first, second = widths_of(features)
        parts = [[(0, first), (features, LANES)], [(first, second)]]
    else:
        parts = [[(0, width)]]

    def kernel(own_ref, came_ref, *merged_refs):
        for ref, part in zip(merged_refs, parts):
            at = 0
            for start, size in part:
                source, target = slice(start, start + size), slice(at, at + size)
                ref[:lights, target] = own_ref[:lights, source]
                ref[lights : 2 * lights, target] = came_ref[:lights, source]
                if heavy:
                    ref[2 * lights :, target] = own_ref[lights:, source] + came_ref[lights:, source]
                at += size

    return pl.pallas_call(
        kernel,
        in_specs=[VMEM] * 2,
        out_specs=[VMEM] * len(parts),
        out_shape=[
            pltpu.VMEM((rows + lights, sum(size for _, size in part)), jnp.bfloat16)
            for part in parts
        ],
        compiler_params=pltpu.CompilerParams(vmem_limit_bytes=4 * MIB),
        name="merge",
    )(own, came)


def places_of(states, group, halves, total, width):
    light = light_rows(total)
    heavy = CAP - light
    phases = group.bit_length() - 1
    each = group // len(states)
    me, half = lax.axis_index("tok"), lax.axis_index("mp")
    counts, owners = [], []
    for chunk in range(group):
        ref = states[chunk // each]
        row = chunk % each * light
        counts.append(ref[row : row + 1, width : width + 1].astype(jnp.float32).astype(jnp.int32))
        moved = 0
        for m in range(halves):
            mask = sum(
                mask_of(p, m, phases) for p in range(phases) if chunk >> p & 1
            )
            moved = moved + jnp.where(half == m, mask, 0)
        owners.append(lax.bitwise_xor(me, moved))
    offsets = []
    for chunk in range(group):
        offset = jnp.zeros_like(counts[0])
        for other in range(group):
            if other != chunk:
                ahead = (owners[other] < owners[chunk]).astype(jnp.int32)
                offset = offset + counts[other] * ahead
        offsets.append(offset)
    first = jnp.zeros_like(counts[0])
    extra = jnp.zeros_like(counts[0])
    for count, offset in zip(counts, offsets):
        first = first + jnp.where(count > light, offset + light, 0)
        extra = extra + jnp.where(count > light, count - light, 0)
    slots = each * light + heavy
    lane = lax.broadcasted_iota(jnp.int32, (1, slots), 1)
    target = lax.broadcasted_iota(jnp.int32, (total, slots), 0)
    places = []
    for state in range(len(states)):
        start = jnp.broadcast_to(first - each * light, (1, slots))
        valid = lane - each * light < extra
        for local in range(each):
            chunk = state * each + local
            here = (lane >= local * light) & (lane < (local + 1) * light)
            start = jnp.where(here, offsets[chunk] - local * light, start)
            valid = jnp.where(here, (lane - local * light < counts[chunk]).astype(jnp.int32), valid.astype(jnp.int32)) > 0
        wanted = jnp.where(valid, start + lane, -1)
        places.append(jnp.where(wanted == target, 1.0, 0.0).astype(jnp.bfloat16))
    return places


def pack_rows(places, state_refs, lhs_ref):
    width = lhs_ref.shape[0]
    packed = None
    for place, ref in zip(places, state_refs):
        one = jnp.dot(place, ref[:, :width], preferred_element_type=jnp.float32)
        packed = one if packed is None else packed + one
    lhs_ref[...] = packed.T.astype(jnp.bfloat16)


def product(lhs_ref, start, stored_ref):
    return jnp.dot(
        lhs_ref[start : start + BLOCK, :], stored_ref[...], preferred_element_type=jnp.float32
    ).astype(jnp.bfloat16)


def send_block(source_ref, start, grad_ref, base, sem):
    copy = pltpu.make_async_copy(
        source_ref.at[pl.ds(start, BLOCK)], grad_ref.at[pl.ds(base + start, BLOCK)], sem
    )
    copy.start()
    return copy


def first_gradient(states, stored, features, group, halves):
    width = states[0].shape[1] - LANES
    total, hidden = stored.shape
    slots = states[0].shape[0]
    left = min(LEFT * BLOCK, width - BLOCK)
    sent = width - left

    def kernel(*refs):
        state_refs = refs[: len(states)]
        stored_ref, grad_ref, place_ref, spare_ref, lhs_ref, held_ref, sems = refs[len(states) :]
        places = places_of(state_refs, group, halves, total, width)
        for index, place in enumerate(places):
            place_ref[index] = place
        pack_rows(places, state_refs, lhs_ref)
        copies = []
        for index, start in enumerate(range(0, sent, BLOCK)):
            held_ref[start : start + BLOCK, :] = product(lhs_ref, start, stored_ref)
            copies.append(send_block(held_ref, start, grad_ref, 0, sems.at[index]))
        for start in range(sent, width, BLOCK):
            spare_ref[start - sent : start - sent + BLOCK, :] = product(lhs_ref, start, stored_ref)
        for copy in copies:
            copy.wait()

    return pl.pallas_call(
        kernel,
        in_specs=[VMEM] * (len(states) + 1),
        out_specs=[ANY, VMEM, VMEM],
        out_shape=[
            jax.ShapeDtypeStruct((features, hidden), jnp.bfloat16),
            pltpu.VMEM((len(states), total, slots), jnp.bfloat16),
            pltpu.VMEM((left, hidden), jnp.bfloat16),
        ],
        scratch_shapes=[
            pltpu.VMEM((width, total), jnp.bfloat16),
            pltpu.VMEM((sent, hidden), jnp.bfloat16),
            pltpu.SemaphoreType.DMA((sent // BLOCK,)),
        ],
        compiler_params=pltpu.CompilerParams(vmem_limit_bytes=24 * MIB),
        name="gradient0",
    )(*states, stored)


def second_gradient(states, stored, gradient, place, spare):
    width = states[0].shape[1]
    total, hidden = stored.shape
    features = gradient.shape[0]
    base = features - width
    left = spare.shape[0]

    def kernel(*refs):
        state_refs = refs[: len(states)]
        stored_ref, place_ref, spare_ref, _, grad_ref, lhs_ref, held_ref, sems = refs[
            len(states) :
        ]
        copies = []
        for index, start in enumerate(range(0, left, BLOCK)):
            copies.append(send_block(spare_ref, start, grad_ref, base - left, sems.at[index]))
        pack_rows([place_ref[index] for index in range(len(states))], state_refs, lhs_ref)
        for index, start in enumerate(range(0, width, BLOCK), left // BLOCK):
            held_ref[start : start + BLOCK, :] = product(lhs_ref, start, stored_ref)
            copies.append(send_block(held_ref, start, grad_ref, base, sems.at[index]))
        for copy in copies:
            copy.wait()

    return pl.pallas_call(
        kernel,
        in_specs=[VMEM] * (len(states) + 3) + [ANY],
        out_specs=ANY,
        out_shape=jax.ShapeDtypeStruct(gradient.shape, jnp.bfloat16),
        input_output_aliases={len(states) + 3: 0},
        scratch_shapes=[
            pltpu.VMEM((width, total), jnp.bfloat16),
            pltpu.VMEM((width, hidden), jnp.bfloat16),
            pltpu.SemaphoreType.DMA(((left + width) // BLOCK,)),
        ],
        compiler_params=pltpu.CompilerParams(vmem_limit_bytes=24 * MIB),
        name="gradient1",
    )(*states, stored, place, spare, gradient)


def per_device(out_cotangent, block_output, router_logits, keep_flags, router_weight, activated):
    cotangent = out_cotangent[0]
    stored = activated[0]
    segments = lax.axis_size("segment")
    group = lax.axis_size("tok")
    halves = lax.axis_size("mp")
    back = [(i, i - 1) for i in range(1, segments)]

    phases = group.bit_length() - 1
    light = light_rows(stored.shape[0])

    def exchange(rows, phase):
        pairs = [
            (t * halves + m, (t ^ mask_of(phase, m, phases)) * halves + m)
            for t in range(group)
            for m in range(halves)
        ]
        return lax.ppermute(rows, ("tok", "mp"), pairs)

    rows, score, weight, held, cot = prepare(
        cotangent, block_output[0], router_logits, keep_flags, router_weight, stored
    )
    scores = [score] + [
        lax.ppermute(score, "mp", [(i, (i + r) % halves) for i in range(halves)])
        for r in range(1, halves)
    ]
    dx = input_gradient(cot, scores, weight)
    received = lax.ppermute(dx, "segment", back)
    for phase in range(phases - 1):
        came = exchange(rows, phase)
        merged = merge(rows, came, light, phase == phases - 2)
        rows = merged[0]
    pieces = [[rows, exchange(rows, phases - 1)] for rows in merged]
    gradient, place, spare = first_gradient(pieces[0], held, cotangent.shape[1], group, halves)
    gradient = second_gradient(pieces[1], held, gradient, place, spare)
    return (received[None], gradient[None])


def solution(mesh):
    in_specs = (
        P("segment", "tok", "mp"),
        P("segment", "tok", "mp"),
        P("segment", "tok"),
        P("segment", "tok"),
        P("segment", "mp"),
        P("segment", None, "tok"),
    )
    out_specs = (P("segment", "tok", "mp"), P("segment", "mp", "tok"))
    return jax.shard_map(
        per_device, mesh=mesh, in_specs=in_specs, out_specs=out_specs, check_vma=False
    )
```

time: 33.8 us -> 26.5 us (0.78)
  starting transfers between devices: 12.7 us -> 6.92 us
  waiting for transfers between devices: 10.6 us -> 9.32 us
  other arithmetic: 1.04 us -> 0 us
  local copies, waits for them, and re-layouts: 0.01 us -> 0.8 us
    ppermute x9 -> x5, starting transfers between devices: 12.7 us -> 6.92 us  [the longest x3 5.07 us: exchange(): return lax.ppermute(rows, ('tok', 'mp'), pairs)]
    ppermute x9 -> x5, waiting for transfers between devices: 10.6 us -> 9.32 us  [the longest x3 8.5 us: exchange(): return lax.ppermute(rows, ('tok', 'mp'), pairs)]
    broadcast_in_dim x1 -> x0, other arithmetic: 1.03 us -> none  [per_device(): return (received[None], gradient[None])]
    unnamed x0 -> x1, local copies, waits for them, and re-layouts: none -> 0.8 us
    pallas_call x3 -> x5, Pallas kernels: 8.53 us -> 8.56 us  [the longest x1 4.5 us: second_gradient(): pl.pallas_call(kernel, in_specs=[VMEM] * (len(states) + 3) + [ANY], out_s...]
  transfers between devices with their start and end apart: 9 -> 5, of which waited for: 1 -> 3; matrix products, arithmetic and copies ran while one was open for 0% -> 0% of each run, Pallas kernels for 21% -> 26%
where the time goes in v2:
time: 26.5 us; the launch traced here: 26.3 us
  waiting for transfers between devices  9.32 us (35%)
  Pallas kernels  8.56 us (32%)
  starting transfers between devices  6.92 us (26%)
  local copies, waits for them, and re-layouts  0.8 us (3%)
  between operations  0.69 us (3%)
    ppermute x3, waiting for transfers between devices, exchange(): return lax.ppermute(rows, ('tok', 'mp'), pairs)  8.5 us
    ppermute x3, starting transfers between devices, exchange(): return lax.ppermute(rows, ('tok', 'mp'), pairs)  5.07 us
    pallas_call x1, Pallas kernels, second_gradient(): pl.pallas_call(kernel, in_specs=[VMEM] * (len(states) + 3) + [ANY], out_s...  4.5 us
    pallas_call x1, Pallas kernels, first_gradient(): pl.pallas_call(kernel, in_specs=[VMEM] * (len(states) + 1), out_specs=[AN...  2.25 us
    pallas_call x1, Pallas kernels, prepare(): pl.pallas_call(prepare_kernel, in_specs=[HBM] * 6, out_specs=[VMEM] * 5,...  1.59 us
    ppermute x1, starting transfers between devices, per_device(): received = lax.ppermute(dx, 'segment', back)  1.29 us
    ppermute x1, waiting for transfers between devices, per_device(): lax.ppermute(score, 'mp', [(i, (i + r) % halves) for i in range(halves)])  0.82 us
    unnamed x1, local copies, waits for them, and re-layouts  0.8 us
  transfers between devices with their start and end apart: 5, of which 3 were waited for; matrix products, arithmetic and copies ran while one was open for 0% of the time, Pallas kernels for 26%

profile of v2, /device:TPU:0, one launch (start us, length us, event | category | flops | bytes accessed | tf_op | source)
XLA Modules:
  0.0 26.3 jit_solution(6674859390775814485)
XLA Ops:
  0.6 1.6 %prepare.1 = (bf16[48,2176]{1,0:T(8,128)(2,1)S(1)}, f32[1,128]{1,0:T(1,128)S(1)}, f32[1,2048]{1,0:T(1,128)S(1)}, bf16[64,3584]{1,0:T(8,128)(2,1)S(1)}, bf16[128,2048]{1,0:T(8,128)(2,1)S(1)}) custom-call(bf16[128,2048]{1,0:T(8,128)(2,1)} %bitcast.7, bf16[128,2048]{1,0:T(8,128)(2,1)} %bitcast.8, f32[1,128]{1,0:T(1,128)} %logit_hbm.1, s32[1,128]{1,0:T(1,128)} %keep_hbm.1, ...), custom_call_target="tpu_custom_call" | custom-call | tf_op jit(solution)/shard_map/prepare/pallas_call | solution.py:73
  2.2 0.6 %collective-permute-start = (f32[1,128]{1,0:T(1,128)S(1)}, f32[1,128]{1,0:T(1,128)S(1)}, u32[]{:S(2)}, u32[]{:S(2)}) collective-permute-start(f32[1,128]{1,0:T(1,128)S(1)} %get-tuple-element.14.refs_0_), channel_id=1, source_target_pairs={{0,1},{1,0},{2,3},{3,2},{4,5},{5,4},{6,7},{7,6},{8,9},{9,8},{10,11... | collective-permute-start | bytes 1544 | tf_op jit(solution)/shard_map/ppermute | solution.py:342
  2.8 0.8 %collective-permute-done.refs_1_ = f32[1,128]{1,0:T(1,128)S(1)} collective-permute-done((f32[1,128]{1,0:T(1,128)S(1)}, f32[1,128]{1,0:T(1,128)S(1)}, u32[]{:S(2)}, u32[]{:S(2)}) %collective-permute-start) | collective-permute-done | bytes 544 | tf_op jit(solution)/shard_map/ppermute | solution.py:342
  3.6 0.2 input_gradient.1
  3.8 1.3 %collective-permute-start.1 = (bf16[128,2048]{1,0:T(8,128)(2,1)S(1)}, bf16[128,2048]{1,0:T(8,128)(2,1)S(1)}, u32[]{:S(2)}, u32[]{:S(2)}) collective-permute-start(bf16[128,2048]{1,0:T(8,128)(2,1)S(1)} %input_gradient.1), channel_id=1, source_target_pairs={{8,0},{16,8},{24,16},{9,1},{17,9},{25,17},{10,2},{18,10},{26,18},{... | collective-permute-start | bytes 1572872 | tf_op jit(solution)/shard_map/ppermute | solution.py:346
  5.1 2.9 %collective-permute-start.2 = (bf16[48,2176]{1,0:T(8,128)(2,1)S(1)}, bf16[48,2176]{1,0:T(8,128)(2,1)S(1)}, u32[]{:S(2)}, u32[]{:S(2)}) collective-permute-start(bf16[48,2176]{1,0:T(8,128)(2,1)S(1)} %get-tuple-element.15.own_ref), channel_id=1, source_target_pairs={{0,2},{1,5},{2,0},{3,7},{4,6},{5,1},{6,4},{7,3},{8,10},{9,13},{10,... | collective-permute-start | bytes 626696 | tf_op jit(solution)/shard_map/ppermute | solution.py:336
  8.0 3.8 %collective-permute-done.2.came_ref = bf16[48,2176]{1,0:T(8,128)(2,1)S(1)} collective-permute-done((bf16[48,2176]{1,0:T(8,128)(2,1)S(1)}, bf16[48,2176]{1,0:T(8,128)(2,1)S(1)}, u32[]{:S(2)}, u32[]{:S(2)}) %collective-permute-start.2) | collective-permute-done | bytes 208928 | tf_op jit(solution)/shard_map/ppermute | solution.py:336
  11.8 2.1 %collective-permute-start.3 = (bf16[64,1280]{1,0:T(8,128)(2,1)S(1)}, bf16[64,1280]{1,0:T(8,128)(2,1)S(1)}, u32[]{:S(2)}, u32[]{:S(2)}) collective-permute-start(bf16[64,1280]{1,0:T(8,128)(2,1)S(1)} %get-tuple-element.16.refs_0_), channel_id=1, source_target_pairs={{0,4},{1,3},{2,6},{3,1},{4,0},{5,7},{6,2},{7,5},{8,12},{9,11},{10,... | collective-permute-start | bytes 491528 | tf_op jit(solution)/shard_map/ppermute | solution.py:336
  13.9 0.1 collective-permute-start.4
  14.0 4.7 %collective-permute-done.4.refs_1_ = bf16[64,896]{1,0:T(8,128)(2,1)S(1)} collective-permute-done((bf16[64,896]{1,0:T(8,128)(2,1)S(1)}, bf16[64,896]{1,0:T(8,128)(2,1)S(1)}, u32[]{:S(2)}, u32[]{:S(2)}) %collective-permute-start.4) | collective-permute-done | bytes 114720 | tf_op jit(solution)/shard_map/ppermute | solution.py:336
  18.7 2.3 %gradient0.1 = (bf16[2048,3584]{1,0:T(8,128)(2,1)}, bf16[2,64,64]{2,1,0:T(8,128)(2,1)S(1)}, bf16[384,3584]{1,0:T(8,128)(2,1)S(1)}) custom-call(bf16[64,896]{1,0:T(8,128)(2,1)S(1)} %get-tuple-element.18.refs_0_, bf16[64,896]{1,0:T(8,128)(2,1)S(1)} %collective-permute-done.4.refs_1_, bf16[64,3584]{1,0:T(8,128)(2,1)S(1)} %get-tuple-element.17.refs_2_), custom_call_target="tpu_custom_call" | custom-call | tf_op jit(solution)/shard_map/gradient0/pallas_call | solution.py:262
  21.0 0.0 collective-permute-done.3.refs_1_
  21.0 4.5 %gradient1.1 = bf16[2048,3584]{1,0:T(8,128)(2,1)} custom-call(bf16[64,1280]{1,0:T(8,128)(2,1)S(1)} %get-tuple-element.16.refs_0_, bf16[64,1280]{1,0:T(8,128)(2,1)S(1)} %collective-permute-done.3.refs_1_, bf16[64,3584]{1,0:T(8,128)(2,1)S(1)} %get-tuple-element.17.refs_2_, ...), custom_call_target="tpu_custom_call", output_to_operand_aliasing={{}: (5, {})} | custom-call | tf_op jit(solution)/shard_map/gradient1/pallas_call | solution.py:303
  25.5 0.0 collective-permute-done.1
  25.5 0.8 %copy.11 = bf16[1,128,2048]{2,1,0:T(8,128)(2,1)} copy(bf16[1,128,2048]{2,1,0:T(8,128)(2,1)S(1)} %bitcast.6) | data formatting | bytes 1048576
  (1 shorter events, 0.0 us)
Async XLA Ops:
  2.2 1.4 %collective-permute-start = (f32[1,128]{1,0:T(1,128)S(1)}, f32[1,128]{1,0:T(1,128)S(1)}, u32[]{:S(2)}, u32[]{:S(2)}) collective-permute-start(f32[1,128]{1,0:T(1,128)S(1)} %get-tuple-element.14.refs_0_), channel_id=1, source_target_pairs={{0,1},{1,0},{2,3},{3,2},{4,5},{5,4},{6,7},{7,6},{8,9},{9,8},{10,11... | collective-permute-start | bytes 1544 | tf_op jit(solution)/shard_map/ppermute | solution.py:342
  3.8 21.7 %collective-permute-start.1 = (bf16[128,2048]{1,0:T(8,128)(2,1)S(1)}, bf16[128,2048]{1,0:T(8,128)(2,1)S(1)}, u32[]{:S(2)}, u32[]{:S(2)}) collective-permute-start(bf16[128,2048]{1,0:T(8,128)(2,1)S(1)} %input_gradient.1), channel_id=1, source_target_pairs={{8,0},{16,8},{24,16},{9,1},{17,9},{25,17},{10,2},{18,10},{26,18},{... | collective-permute-start | bytes 1572872 | tf_op jit(solution)/shard_map/ppermute | solution.py:346
  5.1 6.7 %collective-permute-start.2 = (bf16[48,2176]{1,0:T(8,128)(2,1)S(1)}, bf16[48,2176]{1,0:T(8,128)(2,1)S(1)}, u32[]{:S(2)}, u32[]{:S(2)}) collective-permute-start(bf16[48,2176]{1,0:T(8,128)(2,1)S(1)} %get-tuple-element.15.own_ref), channel_id=1, source_target_pairs={{0,2},{1,5},{2,0},{3,7},{4,6},{5,1},{6,4},{7,3},{8,10},{9,13},{10,... | collective-permute-start | bytes 626696 | tf_op jit(solution)/shard_map/ppermute | solution.py:336
  11.8 9.2 %collective-permute-start.3 = (bf16[64,1280]{1,0:T(8,128)(2,1)S(1)}, bf16[64,1280]{1,0:T(8,128)(2,1)S(1)}, u32[]{:S(2)}, u32[]{:S(2)}) collective-permute-start(bf16[64,1280]{1,0:T(8,128)(2,1)S(1)} %get-tuple-element.16.refs_0_), channel_id=1, source_target_pairs={{0,4},{1,3},{2,6},{3,1},{4,0},{5,7},{6,2},{7,5},{8,12},{9,11},{10,... | collective-permute-start | bytes 491528 | tf_op jit(solution)/shard_map/ppermute | solution.py:336
  13.9 4.8 %collective-permute-start.4 = (bf16[64,896]{1,0:T(8,128)(2,1)S(1)}, bf16[64,896]{1,0:T(8,128)(2,1)S(1)}, u32[]{:S(2)}, u32[]{:S(2)}) collective-permute-start(bf16[64,896]{1,0:T(8,128)(2,1)S(1)} %get-tuple-element.18.refs_0_), channel_id=1, source_target_pairs={{0,4},{1,3},{2,6},{3,1},{4,0},{5,7},{6,2},{7,5},{8,12},{9,11},{10,... | collective-permute-start | bytes 344072 | tf_op jit(solution)/shard_map/ppermute | solution.py:336
